TPU v7x, 32 devices: a whole 2x2x4 slice. The times are simulated.
32 devices in a mesh: rep: 4 (over y, x), fsdp: 8 (over z, core).
Axes of the slice: x: 2, y: 2, z: 4, core: 2. Of those that a mesh axis runs over, the one named last changes fastest.
Arguments:
- momentum: float32 [4, 18432, 2304], P('rep', 'fsdp'), may hold values from -60 to 60
- gradient: bfloat16 [4, 18432, 2304], P('rep', 'fsdp'), may hold values from -30 to 30
- right_factor: float32 [2304, 256], P('fsdp'), may hold values from -0.125 to 0.125
Outputs:
- new_momentum: float32 [4, 18432, 2304], P('rep', 'fsdp')
- update: bfloat16 [18432, 2304], P('fsdp')
- new_factor: float32 [2304, 256], P('fsdp')
All inputs are finite; a program needn't handle non-finite values.
Results may differ from a plain program's by a relative error of at most 0.001.
Values sent between devices are 32-bit elements; how exact they have to be, the bound alone decides.
A program may use at most 128 MiB of HBM per device.

v0:
```python
import math
import jax
import jax.numpy as jnp
from jax import lax
from jax.sharding import PartitionSpec as P

ROWS = 18432
COLS = 2304
RANK = 256
epsilon = 1e-06
decay_rate = 0.95
highest = lax.Precision.HIGHEST


def shards(momentum, gradient, right_factor):
    buffer = momentum[0] + gradient[0].astype(jnp.float32)
    replicas = lax.axis_size("rep")
    columns = buffer
    partial_left = jnp.dot(
        columns,
        lax.all_gather(right_factor, "fsdp", axis=0, tiled=True),
        precision=highest,
        preferred_element_type=jnp.float32,
    )
    projected = lax.psum(partial_left, "rep")
    local_gram = jnp.dot(
        projected.T, projected, precision=highest, preferred_element_type=jnp.float32
    )
    gram_matrix = lax.psum(local_gram, "fsdp")
    lower_factor = jnp.linalg.cholesky(gram_matrix)
    orthonormal = jax.scipy.linalg.solve_triangular(lower_factor, projected.T, lower=True).T
    columns = buffer
    scattered = lax.psum_scatter(
        lax.dot_general(
            columns,
            orthonormal,
            (((0,), (0,)), ((), ())),
            precision=highest,
            preferred_element_type=jnp.float32,
        ),
        "fsdp",
        scatter_dimension=0,
        tiled=True,
    )
    own_factor = lax.psum(scattered, "rep") / replicas
    full_factor = lax.all_gather(own_factor, "fsdp", axis=0, tiled=True)
    col_norms = jnp.sqrt(jnp.sum(full_factor * full_factor, axis=0) + epsilon)
    new_factor = own_factor / col_norms
    correction = lax.dot_general(
        orthonormal,
        full_factor,
        (((1,), (1,)), ((), ())),
        precision=highest,
        preferred_element_type=jnp.float32,
    )
    new_momentum = (buffer - (1.0 - decay_rate) * correction)[None]
    direction = lax.dot_general(
        orthonormal,
        full_factor / col_norms,
        (((1,), (1,)), ((), ())),
        precision=highest,
        preferred_element_type=jnp.float32,
    )
    update = (math.sqrt(ROWS * COLS / RANK) * direction).astype(jnp.bfloat16)
    return (new_momentum, update, new_factor)


def solution(mesh):
    in_specs = (P("rep", "fsdp", None), P("rep", "fsdp", None), P("fsdp", None))
    out_specs = (P("rep", "fsdp", None), P("fsdp", None), P("fsdp", None))
    return jax.shard_map(shards, mesh=mesh, in_specs=in_specs, out_specs=out_specs, check_vma=False)
```

profile of v0, /device:TPU:0, one launch (start us, length us, event | category | flops | bytes accessed | tf_op | source)
XLA Modules:
  0.0 512.4 jit_solution(980822565762107197)
XLA Ops:
  7.2 0.0 all-gather.3.cloned.1.call-start
  7.2 0.7 all-gather.3.cloned.1.call-update
  7.9 0.0 all-reduce.5.cloned.1.call-start
  7.9 35.9 %all-gather.3.cloned.1.call-done = f32[2304,256]{1,0:T(8,128)} async-done(((f32[288,256]{1,0:T(8,128)}), f32[2304,256]{1,0:T(8,128)}) %all-gather.3.cloned.1.call-update) | async-done | bytes 2359312 | tf_op jit(solution)/shard_map/all_gather | solution.py:21
  43.8 22.8 %fusion.3 = f32[2304,256]{1,0:T(8,128)} fusion(f32[2304,256]{1,0:T(8,128)} %all-gather.3.cloned.1.call-done, f32[1,2304,2304]{2,1,0:T(8,128)} %param.3, bf16[1,2304,2304]{2,1,0:T(8,128)(2,1)} %param.4), kind=kOutput, calls=%fused_computation.7 | convolution fusion | flops 16318070784 | bytes 36569088 | tf_op jit(solution)/shard_map/dot_general | solution.py:19
  66.6 0.0 all-reduce.5.cloned.1.call-update
  66.6 0.0 all-reduce.7.cloned.1.call-start
  66.7 73.2 %all-reduce.5.cloned.1.call-done = f32[2304,256]{1,0:T(8,128)} async-done(((f32[2304,256]{1,0:T(8,128)}), f32[2304,256]{1,0:T(8,128)}) %all-reduce.5.cloned.1.call-update) | async-done | bytes 2359312 | tf_op jit(solution)/shard_map/psum | solution.py:25
  139.9 6.9 %fusion.21 = f32[256,256]{0,1:T(8,128)} fusion(f32[2304,256]{1,0:T(8,128)} %all-reduce.5.cloned.1.call-done), kind=kOutput, calls=%fused_computation.48 | convolution fusion | flops 1811939328 | bytes 2621440 | tf_op jit(solution)/shard_map/dot_general | solution.py:26
  146.8 0.0 all-reduce.7.cloned.1.call-update
  146.9 0.3 reduce-scatter.2.cloned.1.call-start
  147.1 55.3 %all-reduce.7.cloned.1.call-done = f32[256,256]{0,1:T(8,128)} async-done(((f32[256,256]{0,1:T(8,128)}), f32[256,256]{0,1:T(8,128)}) %all-reduce.7.cloned.1.call-update) | async-done | bytes 262160 | tf_op jit(solution)/shard_map/psum | solution.py:29
  202.4 1.1 copy.7
  203.5 1.0 fusion.11
  204.5 11.7 %cholesky.50 = f32[128,128]{1,0:T(8,128)S(1)} custom-call(f32[128,128]{1,0:T(8,128)S(1)} %cholesky.118), custom_call_target="Cholesky" | custom-call | tf_op jit(solution)/shard_map/jit(cholesky)/cholesky | solution.py:30
  216.3 9.8 %custom-call.15 = f32[1,128,128]{1,2,0:T(8,128)S(1)} custom-call(f32[1,128,128]{2,1,0:T(8,128)S(1)} %get-tuple-element.24), custom_call_target="InvertDiagBlocksLowerTriangular" | custom-call | tf_op jit(solution)/shard_map/jit(cholesky)/cholesky | solution.py:30
  226.1 0.2 constant_dynamic-update-slice_fusion.1
  226.3 0.3 convolution_subtract_fusion.1
  226.6 11.7 %cholesky.105 = f32[128,128]{1,0:T(8,128)S(1)} custom-call(f32[128,128]{1,0:T(8,128)S(1)} %convolution_subtract_fusion.1), custom_call_target="Cholesky" | custom-call | tf_op jit(solution)/shard_map/jit(cholesky)/cholesky | solution.py:30
  238.3 0.6 compare_reduce_fusion
  240.3 0.1 triangular_solve.57
  240.4 4.4 while.1
  240.8 0.6 fusion.31
  241.4 1.4 bitcast_dynamic-update-slice_fusion.2
  242.8 0.6 fusion.31
  243.4 1.4 bitcast_dynamic-update-slice_fusion.2
  244.8 0.0 copy-start.1
  244.8 20.3 %custom-call.16 = f32[2,128,128]{1,2,0:T(8,128)} custom-call(f32[2,128,128]{2,1,0:T(8,128)S(1)} %get-tuple-element.10), custom_call_target="InvertDiagBlocksLowerTriangular" | custom-call | tf_op jit(solution)/shard_map/jit(_solve_triangular)/triangular_solve | solution.py:31
  265.1 2.0 fusion.8
  267.1 0.0 copy-start.3
  267.1 2.9 convolution_subtract_fusion
  270.0 1.2 fusion.13
  271.2 38.5 %fusion.1 = f32[2304,256]{1,0:T(8,128)} fusion(f32[1,2304,2304]{2,1,0:T(8,128)} %param.3, bf16[1,2304,2304]{2,1,0:T(8,128)(2,1)} %param.4, f32[128,2304]{1,0:T(8,128)S(1)} %fusion.13, f32[128,2304]{1,0:T(8,128)S(1)} %fusion.8), kind=kOutput, calls=%fused_computation.5 | convolution fusion | flops 16318660608 | bytes 36569088 | tf_op jit(solution)/shard_map/dot_general | solution.py:34
  309.7 0.0 reduce-scatter.2.cloned.1.call-update
  309.7 0.0 all-reduce.9.cloned.1.call-start
  309.7 36.2 %reduce-scatter.2.cloned.1.call-done = f32[288,256]{1,0:T(8,128)} async-done(((f32[2304,256]{1,0:T(8,128)}), f32[288,256]{1,0:T(8,128)}) %reduce-scatter.2.cloned.1.call-update) | async-done | bytes 294928 | tf_op jit(solution)/shard_map/reduce_scatter | solution.py:33
  345.9 0.0 all-reduce.9.cloned.1.call-update
  346.0 0.0 all-gather.5.cloned.1.call-start
  346.0 45.0 %all-reduce.9.cloned.1.call-done = f32[288,256]{1,0:T(8,128)} async-done(((f32[288,256]{1,0:T(8,128)}), f32[288,256]{1,0:T(8,128)}) %all-reduce.9.cloned.1.call-update) | async-done | bytes 294928 | tf_op jit(solution)/shard_map/psum | solution.py:45
  391.0 1.8 broadcast_multiply_fusion
  392.8 0.0 all-gather.5.cloned.1.call-update
  392.8 31.8 %all-gather.5.cloned.1.call-done = f32[2304,256]{1,0:T(8,128)} async-done(((f32[288,256]{1,0:T(8,128)}), f32[2304,256]{1,0:T(8,128)}) %all-gather.5.cloned.1.call-update) | async-done | bytes 2359312 | tf_op jit(solution)/shard_map/all_gather | solution.py:46
  424.5 2.1 multiply_reduce_fusion
  426.7 0.0 copy-done.2
  426.7 0.7 broadcast_divide_fusion
  427.4 36.8 %fusion.6 = bf16[2304,2304]{1,0:T(8,128)(2,1)} fusion(f32[2304,256]{1,0:T(8,128)} %all-gather.5.cloned.1.call-done, f32[128,2304]{1,0:T(8,128)S(1)} %fusion.13, f32[128,2304]{1,0:T(8,128)S(1)} %fusion.8, f32[256]{0:T(256)S(1)} %add_sqrt_fusion), kind=kOutput, calls=%fused_computation.11 | convolution fusion | flops 16319250432 | bytes 15336448 | tf_op jit(solution)/shard_map/dot_general | solution.py:57
  464.3 0.0 slice-done
  464.3 40.8 %fusion.5 = f32[1,2304,2304]{2,1,0:T(8,128)} fusion(f32[2304,256]{1,0:T(8,128)} %all-gather.5.cloned.1.call-done, f32[1,2304,2304]{2,1,0:T(8,128)} %param.3, bf16[1,2304,2304]{2,1,0:T(8,128)(2,1)S(1)} %bitcast.47, f32[128,2304]{1,0:T(8,128)S(1)} %fusion.13, f32[128,2304]{1,0:T(8,128)S(1)} %fusion.8), kind=kOutput, calls=%fused_computation.10 | convolution fusion | flops 16329277440 | bytes 57802752 | tf_op jit(solution)/shard_map/dot_general | solution.py:49
  (21 shorter events, 0.2 us)
Async XLA Ops:
  7.2 36.6 %all-gather.3.cloned.1.call-start = ((), (), s32[]{:S(2)}) async-start(), calls=%async_computation.1 | async-start | bytes 2654208 | tf_op jit(solution)/shard_map/all_gather | solution.py:21
  7.9 132.0 %all-reduce.5.cloned.1.call-start = ((), (), s32[]{:S(2)}) async-start(), calls=%async_computation.2 | async-start | bytes 4718592 | tf_op jit(solution)/shard_map/psum | solution.py:25
  66.6 135.8 %all-reduce.7.cloned.1.call-start = ((), (), s32[]{:S(2)}) async-start(), calls=%async_computation.3 | async-start | bytes 524288 | tf_op jit(solution)/shard_map/psum | solution.py:29
  146.8 118.3 %copy-start = (f32[2304,256]{1,0:T(8,128)S(1)}, f32[2304,256]{1,0:T(8,128)}, u32[]{:S(2)}) copy-start(f32[2304,256]{1,0:T(8,128)} %all-reduce.5.cloned.1.call-done) | copy-start | bytes 7077892
  146.9 199.1 %reduce-scatter.2.cloned.1.call-start = ((), (), s32[]{:S(2)}) async-start(), calls=%async_computation.4 | async-start | bytes 2654208 | tf_op jit(solution)/shard_map/reduce_scatter | solution.py:33
  244.8 20.3 %copy-start.1 = (f32[256,256]{1,0:T(8,128)}, f32[256,256]{1,0:T(8,128)S(1)}, u32[]{:S(2)}) copy-start(f32[256,256]{1,0:T(8,128)S(1)} %get-tuple-element.86) | copy-start | bytes 786436
  267.1 2.9 copy-start.3
  309.7 81.3 %all-reduce.9.cloned.1.call-start = ((), (), s32[]{:S(2)}) async-start(), calls=%async_computation.5 | async-start | bytes 589824 | tf_op jit(solution)/shard_map/psum | solution.py:45
  346.0 78.6 %all-gather.5.cloned.1.call-start = ((), (), s32[]{:S(2)}) async-start(), calls=%async_computation.6 | async-start | bytes 2654208 | tf_op jit(solution)/shard_map/all_gather | solution.py:46
  391.0 35.7 %copy-start.2 = (f32[288,256]{1,0:T(8,128)S(1)}, f32[288,256]{1,0:T(8,128)}, u32[]{:S(2)}) copy-start(f32[288,256]{1,0:T(8,128)} %all-reduce.9.cloned.1.call-done) | copy-start | bytes 884740
  424.5 39.7 %slice-start = ((s8[10616832]{0:T(1024)(128)(4,1)}), s8[4194304]{0:T(1024)(128)(4,1)S(1)}, s32[]{:S(2)}) async-start(s8[10616832]{0:T(1024)(128)(4,1)} %bitcast.46), calls=%async_computation.7 | async-start | bytes 8388608
  427.4 36.8 %slice-start.1 = ((s8[10616832]{0:T(1024)(128)(4,1)}), s8[4194304]{0:T(1024)(128)(4,1)S(1)}, s32[]{:S(2)}) async-start(s8[10616832]{0:T(1024)(128)(4,1)} %bitcast.46), calls=%async_computation.8 | async-start | bytes 8388608
  427.4 36.8 %slice-start.2 = ((s8[10616832]{0:T(1024)(128)(4,1)}), s8[2228224]{0:T(1024)(128)(4,1)S(1)}, s32[]{:S(2)}) async-start(s8[10616832]{0:T(1024)(128)(4,1)} %bitcast.46), calls=%async_computation.9 | async-start | bytes 4456448
Sparse Core Ops, SparseCore 0:
  9.6 34.1 all-gather.2
  66.8 73.0 all-reduce.4
  147.0 55.4 all-reduce.6
  309.8 36.0 reduce-scatter.1
  348.7 42.2 all-reduce.8
  393.1 31.4 all-gather.4
where the time goes:
time: 520 us; the launch traced here: 512 us
  waiting for transfers between devices  278 us (53%)
  matrix products  152 us (29%)
  other arithmetic  59.9 us (12%)
  between operations  16 us (3%)
    psum x1, waiting for transfers between devices, shards(): projected = lax.psum(partial_left, 'rep')  73.2 us
    psum x1, waiting for transfers between devices, shards(): gram_matrix = lax.psum(local_gram, 'fsdp')  55.3 us
    psum x1, waiting for transfers between devices, shards(): own_factor = lax.psum(scattered, 'rep') / replicas  45 us
    dot_general x1, matrix products, shards(): lax.dot_general(orthonormal, full_factor, (((1,), (1,)), ((), ())), preci...  40.8 us
    dot_general x1, matrix products, shards(): lax.dot_general(columns, orthonormal, (((0,), (0,)), ((), ())), precision...  38.5 us
    dot_general x1, matrix products, shards(): lax.dot_general(orthonormal, full_factor / col_norms, (((1,), (1,)), ((),...  36.8 us
    reduce_scatter x1, waiting for transfers between devices, shards(): lax.psum_scatter(lax.dot_general(columns, orthonormal, (((0,), (0,)), (()...  36.2 us
    all_gather x1, waiting for transfers between devices, shards(): lax.all_gather(right_factor, 'fsdp', axis=0, tiled=True)  35.9 us
  transfers between devices with their start and end apart: 6, of which 6 were waited for; matrix products, arithmetic and copies ran while one was open for 0% of the time, Pallas kernels for 0%

commit v1 on v0

--- a/solution.py
+++ b/solution.py
@@ -43,7 +43,12 @@
         tiled=True,
     )
     own_factor = lax.psum(scattered, "rep") / replicas
-    full_factor = lax.all_gather(own_factor, "fsdp", axis=0, tiled=True)
+    ring = [own_factor]
+    for hop in range(7):
+        ring.append(lax.ppermute(ring[-1], "fsdp", [(dev, (dev + 1) % 8) for dev in range(8)]))
+    full_factor = jnp.roll(
+        jnp.concatenate(ring[::-1], axis=0), (lax.axis_index("fsdp") + 1) * ring[0].shape[0], axis=0
+    )
     col_norms = jnp.sqrt(jnp.sum(full_factor * full_factor, axis=0) + epsilon)
     new_factor = own_factor / col_norms
     correction = lax.dot_general(

time: 520 us -> 548 us (1.054)
  waiting for transfers between devices: 278 us -> 302 us
  local copies, waits for them, and re-layouts: 5.15 us -> 12.7 us
    ppermute x0 -> x7, waiting for transfers between devices: none -> 56 us  [shards(): lax.ppermute(ring[-1], 'fsdp', [(dev, (dev + 1) % 8) for dev in range(8)])]
    all_gather x1 -> x0, waiting for transfers between devices: 31.8 us -> none  [shards(): full_factor = lax.all_gather(own_factor, 'fsdp', axis=0, tiled=True)]
    unnamed x14 -> x30, local copies, waits for them, and re-layouts: 0.03 us -> 7.53 us
  transfers between devices with their start and end apart: 6 -> 12, of which waited for: 6 -> 12; matrix products, arithmetic and copies ran while one was open for 0% -> 0% of each run, Pallas kernels for 0% -> 0%
where the time goes in v1:
time: 548 us; the launch traced here: 541 us
  waiting for transfers between devices  302 us (55%)
  matrix products  151 us (28%)
  other arithmetic  57.5 us (10%)
  between operations  15.8 us (3%)
  local copies, waits for them, and re-layouts  12.7 us (2%)
    psum x1, waiting for transfers between devices, shards(): projected = lax.psum(partial_left, 'rep')  73.2 us
    ppermute x7, waiting for transfers between devices, shards(): lax.ppermute(ring[-1], 'fsdp', [(dev, (dev + 1) % 8) for dev in range(8)])  56 us
    psum x1, waiting for transfers between devices, shards(): gram_matrix = lax.psum(local_gram, 'fsdp')  55.3 us
    psum x1, waiting for transfers between devices, shards(): own_factor = lax.psum(scattered, 'rep') / replicas  45.1 us
    dot_general x1, matrix products, shards(): lax.dot_general(orthonormal, full_factor, (((1,), (1,)), ((), ())), preci...  40.8 us
    dot_general x1, matrix products, shards(): lax.dot_general(columns, orthonormal, (((0,), (0,)), ((), ())), precision...  38.5 us
    reduce_scatter x1, waiting for transfers between devices, shards(): lax.psum_scatter(lax.dot_general(columns, orthonormal, (((0,), (0,)), (()...  36.2 us
    all_gather x1, waiting for transfers between devices, shards(): lax.all_gather(right_factor, 'fsdp', axis=0, tiled=True)  35.9 us
  transfers between devices with their start and end apart: 12, of which 12 were waited for; matrix products, arithmetic and copies ran while one was open for 0% of the time, Pallas kernels for 0%

profile of v1, /device:TPU:0, one launch (start us, length us, event | category | flops | bytes accessed | tf_op | source)
XLA Modules:
  0.0 540.6 jit_solution(3499361927108548478)
XLA Ops:
  7.2 0.7 all-gather.2.cloned.1.call-update
  7.9 35.9 %all-gather.2.cloned.1.call-done = f32[2304,256]{1,0:T(8,128)} async-done(((f32[288,256]{1,0:T(8,128)}), f32[2304,256]{1,0:T(8,128)}) %all-gather.2.cloned.1.call-update) | async-done | bytes 2359312 | tf_op jit(solution)/shard_map/all_gather | solution.py:21
  43.8 22.8 %fusion.3 = f32[2304,256]{1,0:T(8,128)} fusion(f32[2304,256]{1,0:T(8,128)} %all-gather.2.cloned.1.call-done, f32[1,2304,2304]{2,1,0:T(8,128)} %param.3, bf16[1,2304,2304]{2,1,0:T(8,128)(2,1)} %param.4), kind=kOutput, calls=%fused_computation.7 | convolution fusion | flops 16318070784 | bytes 36569088 | tf_op jit(solution)/shard_map/dot_general | solution.py:19
  66.7 73.2 %all-reduce.5.cloned.1.call-done = f32[2304,256]{1,0:T(8,128)} async-done(((f32[2304,256]{1,0:T(8,128)}), f32[2304,256]{1,0:T(8,128)}) %all-reduce.5.cloned.1.call-update) | async-done | bytes 2359312 | tf_op jit(solution)/shard_map/psum | solution.py:25
  139.9 7.1 %fusion.25 = f32[256,256]{0,1:T(8,128)} fusion(f32[2304,256]{1,0:T(8,128)} %all-reduce.5.cloned.1.call-done), kind=kOutput, calls=%fused_computation.68 | convolution fusion | flops 1811939328 | bytes 2621440 | tf_op jit(solution)/shard_map/dot_general | solution.py:26
  147.0 0.3 reduce-scatter.2.cloned.1.call-start
  147.3 55.3 %all-reduce.7.cloned.1.call-done = f32[256,256]{0,1:T(8,128)} async-done(((f32[256,256]{0,1:T(8,128)}), f32[256,256]{0,1:T(8,128)}) %all-reduce.7.cloned.1.call-update) | async-done | bytes 262160 | tf_op jit(solution)/shard_map/psum | solution.py:29
  202.6 1.1 copy.7
  203.7 1.0 fusion.13
  204.7 11.7 %cholesky.50 = f32[128,128]{1,0:T(8,128)S(1)} custom-call(f32[128,128]{1,0:T(8,128)S(1)} %cholesky.118), custom_call_target="Cholesky" | custom-call | tf_op jit(solution)/shard_map/jit(cholesky)/cholesky | solution.py:30
  216.4 9.8 %custom-call.15 = f32[1,128,128]{1,2,0:T(8,128)S(1)} custom-call(f32[1,128,128]{2,1,0:T(8,128)S(1)} %get-tuple-element.24), custom_call_target="InvertDiagBlocksLowerTriangular" | custom-call | tf_op jit(solution)/shard_map/jit(cholesky)/cholesky | solution.py:30
  226.3 0.2 constant_dynamic-update-slice_fusion.16
  226.5 0.3 convolution_subtract_fusion.1
  226.8 11.7 %cholesky.105 = f32[128,128]{1,0:T(8,128)S(1)} custom-call(f32[128,128]{1,0:T(8,128)S(1)} %convolution_subtract_fusion.1), custom_call_target="Cholesky" | custom-call | tf_op jit(solution)/shard_map/jit(cholesky)/cholesky | solution.py:30
  238.5 0.6 compare_reduce_fusion
  240.5 0.1 triangular_solve.57
  240.6 4.4 while.1
  241.0 0.6 fusion.34
  241.6 1.4 bitcast_dynamic-update-slice_fusion.2
  243.0 0.6 fusion.34
  243.6 1.4 bitcast_dynamic-update-slice_fusion.2
  245.0 20.3 %custom-call.16 = f32[2,128,128]{1,2,0:T(8,128)} custom-call(f32[2,128,128]{2,1,0:T(8,128)S(1)} %get-tuple-element.10), custom_call_target="InvertDiagBlocksLowerTriangular" | custom-call | tf_op jit(solution)/shard_map/jit(_solve_triangular)/triangular_solve | solution.py:31
  265.3 2.1 fusion.10
  267.4 2.9 convolution_subtract_fusion
  270.2 1.2 fusion.15
  271.4 38.5 %fusion.1 = f32[2304,256]{1,0:T(8,128)} fusion(f32[1,2304,2304]{2,1,0:T(8,128)} %param.3, bf16[1,2304,2304]{2,1,0:T(8,128)(2,1)} %param.4, f32[128,2304]{1,0:T(8,128)S(1)} %fusion.15, f32[128,2304]{1,0:T(8,128)S(1)} %fusion.10), kind=kOutput, calls=%fused_computation.5 | convolution fusion | flops 16318660608 | bytes 36569088 | tf_op jit(solution)/shard_map/dot_general | solution.py:34
  309.9 36.2 %reduce-scatter.2.cloned.1.call-done = f32[288,256]{1,0:T(8,128)} async-done(((f32[2304,256]{1,0:T(8,128)}), f32[288,256]{1,0:T(8,128)}) %reduce-scatter.2.cloned.1.call-update) | async-done | bytes 294928 | tf_op jit(solution)/shard_map/reduce_scatter | solution.py:33
  346.2 45.1 %all-reduce.9.cloned.1.call-done = f32[288,256]{1,0:T(8,128)} async-done(((f32[288,256]{1,0:T(8,128)}), f32[288,256]{1,0:T(8,128)}) %all-reduce.9.cloned.1.call-update) | async-done | bytes 294928 | tf_op jit(solution)/shard_map/psum | solution.py:45
  391.3 1.1 broadcast_multiply_fusion
  392.4 7.9 %collective-permute-done = f32[288,256]{1,0:T(8,128)S(1)} collective-permute-done((f32[288,256]{1,0:T(8,128)S(1)}, f32[288,256]{1,0:T(8,128)S(1)}, u32[]{:S(2)}, u32[]{:S(2)}) %collective-permute-start) | collective-permute-done | bytes 294944 | tf_op jit(solution)/shard_map/ppermute | solution.py:48
  400.3 7.9 %collective-permute-done.1 = f32[288,256]{1,0:T(8,128)S(1)} collective-permute-done((f32[288,256]{1,0:T(8,128)S(1)}, f32[288,256]{1,0:T(8,128)S(1)}, u32[]{:S(2)}, u32[]{:S(2)}) %collective-permute-start.1) | collective-permute-done | bytes 294944 | tf_op jit(solution)/shard_map/ppermute | solution.py:48
  408.3 7.9 %collective-permute-done.2 = f32[288,256]{1,0:T(8,128)S(1)} collective-permute-done((f32[288,256]{1,0:T(8,128)S(1)}, f32[288,256]{1,0:T(8,128)S(1)}, u32[]{:S(2)}, u32[]{:S(2)}) %collective-permute-start.2) | collective-permute-done | bytes 294944 | tf_op jit(solution)/shard_map/ppermute | solution.py:48
  416.2 7.9 %collective-permute-done.3 = f32[288,256]{1,0:T(8,128)S(1)} collective-permute-done((f32[288,256]{1,0:T(8,128)S(1)}, f32[288,256]{1,0:T(8,128)S(1)}, u32[]{:S(2)}, u32[]{:S(2)}) %collective-permute-start.3) | collective-permute-done | bytes 294944 | tf_op jit(solution)/shard_map/ppermute | solution.py:48
  424.2 0.7 copy-done.3
  424.9 7.9 %collective-permute-done.4 = f32[288,256]{1,0:T(8,128)S(1)} collective-permute-done((f32[288,256]{1,0:T(8,128)S(1)}, f32[288,256]{1,0:T(8,128)S(1)}, u32[]{:S(2)}, u32[]{:S(2)}) %collective-permute-start.4) | collective-permute-done | bytes 294944 | tf_op jit(solution)/shard_map/ppermute | solution.py:48
  432.8 0.7 copy-done.5
  433.5 8.0 %collective-permute-done.5 = f32[288,256]{1,0:T(8,128)} collective-permute-done((f32[288,256]{1,0:T(8,128)S(1)}, f32[288,256]{1,0:T(8,128)}, u32[]{:S(2)}, u32[]{:S(2)}) %collective-permute-start.5) | collective-permute-done | bytes 294944 | tf_op jit(solution)/shard_map/ppermute | solution.py:48
  441.6 8.3 %collective-permute-done.6 = f32[288,256]{1,0:T(8,128)} collective-permute-done((f32[288,256]{1,0:T(8,128)}, f32[288,256]{1,0:T(8,128)}, u32[]{:S(2)}, u32[]{:S(2)}) %collective-permute-start.6) | collective-permute-done | bytes 294944 | tf_op jit(solution)/shard_map/ppermute | solution.py:48
  449.8 1.0 constant_dynamic-update-slice_fusion.15
  450.8 1.0 constant_dynamic-update-slice_fusion.14
  451.8 1.0 constant_dynamic-update-slice_fusion.13
  452.8 1.0 constant_dynamic-update-slice_fusion.12
  453.9 1.0 constant_dynamic-update-slice_fusion.7
  454.9 1.0 constant_dynamic-update-slice_fusion.6
  456.1 0.4 multiply_reduce_fusion
  456.5 40.8 %fusion.5 = f32[1,2304,2304]{2,1,0:T(8,128)} fusion(f32[1,2304,2304]{2,1,0:T(8,128)} %param.3, bf16[1,2304,2304]{2,1,0:T(8,128)(2,1)} %param.4, f32[4608,256]{1,0:T(8,128)S(1)} %constant_dynamic-update-slice_fusion, s32[]{:T(128)S(6)} %select_n.19, f32[128,2304]{1,0:T(8,128)S(1)} %fusion.15, f32[128,2304]{1,0:T(8,128)S(1)} %fusion.10), kind=kOutput, calls=%fused_computation.10 | convolution fusion | flops 16329277440 | bytes 57802756 | tf_op jit(solution)/shard_map/dot_general | solution.py:54
  497.3 35.6 %fusion.6 = bf16[2304,2304]{1,0:T(8,128)(2,1)} fusion(f32[4608,256]{1,0:T(8,128)S(1)} %constant_dynamic-update-slice_fusion, s32[]{:T(128)S(6)} %select_n.19, f32[128,2304]{1,0:T(8,128)S(1)} %fusion.15, f32[128,2304]{1,0:T(8,128)S(1)} %fusion.10, f32[256]{0:T(256)S(1)} %add_sqrt_fusion), kind=kOutput, calls=%fused_computation.11 | convolution fusion | flops 16319250432 | bytes 15336452 | tf_op jit(solution)/shard_map/dot_general | solution.py:62
  532.9 0.7 broadcast_divide_fusion
  (49 shorter events, 0.7 us)
Async XLA Ops:
  7.2 36.6 %all-gather.2.cloned.1.call-start = ((), (), s32[]{:S(2)}) async-start(), calls=%async_computation.1 | async-start | bytes 2654208 | tf_op jit(solution)/shard_map/all_gather | solution.py:21
  7.9 132.0 %all-reduce.5.cloned.1.call-start = ((), (), s32[]{:S(2)}) async-start(), calls=%async_computation.2 | async-start | bytes 4718592 | tf_op jit(solution)/shard_map/psum | solution.py:25
  66.6 136.0 %all-reduce.7.cloned.1.call-start = ((), (), s32[]{:S(2)}) async-start(), calls=%async_computation.3 | async-start | bytes 524288 | tf_op jit(solution)/shard_map/psum | solution.py:29
  139.9 125.4 %copy-start = (f32[2304,256]{1,0:T(8,128)S(1)}, f32[2304,256]{1,0:T(8,128)}, u32[]{:S(2)}) copy-start(f32[2304,256]{1,0:T(8,128)} %all-reduce.5.cloned.1.call-done) | copy-start | bytes 7077892
  147.0 199.2 %reduce-scatter.2.cloned.1.call-start = ((), (), s32[]{:S(2)}) async-start(), calls=%async_computation.4 | async-start | bytes 2654208 | tf_op jit(solution)/shard_map/reduce_scatter | solution.py:33
  245.0 20.3 %copy-start.2 = (f32[256,256]{1,0:T(8,128)}, f32[256,256]{1,0:T(8,128)S(1)}, u32[]{:S(2)}) copy-start(f32[256,256]{1,0:T(8,128)S(1)} %get-tuple-element.85) | copy-start | bytes 786436
  265.3 5.0 copy-start.7
  309.9 81.3 %all-reduce.9.cloned.1.call-start = ((), (), s32[]{:S(2)}) async-start(), calls=%async_computation.5 | async-start | bytes 589824 | tf_op jit(solution)/shard_map/psum | solution.py:45
  391.3 62.6 %copy-start.1 = (f32[288,256]{1,0:T(8,128)S(1)}, f32[288,256]{1,0:T(8,128)}, u32[]{:S(2)}) copy-start(f32[288,256]{1,0:T(8,128)} %all-reduce.9.cloned.1.call-done) | copy-start | bytes 884740
  392.3 8.0 %collective-permute-start = (f32[288,256]{1,0:T(8,128)S(1)}, f32[288,256]{1,0:T(8,128)S(1)}, u32[]{:S(2)}, u32[]{:S(2)}) collective-permute-start(f32[288,256]{1,0:T(8,128)S(1)} %broadcast_multiply_fusion), channel_id=1, source_target_pairs={{0,1},{1,2},{2,3},{3,4},{4,5},{5,6},{6,7},{7,0},{8,9},{9,10},{10,1... | collective-permute-start | bytes 884744 | tf_op jit(solution)/shard_map/ppermute | solution.py:48
  400.3 7.9 %collective-permute-start.1 = (f32[288,256]{1,0:T(8,128)S(1)}, f32[288,256]{1,0:T(8,128)S(1)}, u32[]{:S(2)}, u32[]{:S(2)}) collective-permute-start(f32[288,256]{1,0:T(8,128)S(1)} %collective-permute-done), channel_id=1, source_target_pairs={{0,1},{1,2},{2,3},{3,4},{4,5},{5,6},{6,7},{7,0},{8,9},{9,10},{10,1... | collective-permute-start | bytes 884744 | tf_op jit(solution)/shard_map/ppermute | solution.py:48
  408.3 7.9 %collective-permute-start.2 = (f32[288,256]{1,0:T(8,128)S(1)}, f32[288,256]{1,0:T(8,128)S(1)}, u32[]{:S(2)}, u32[]{:S(2)}) collective-permute-start(f32[288,256]{1,0:T(8,128)S(1)} %collective-permute-done.1), channel_id=1, source_target_pairs={{0,1},{1,2},{2,3},{3,4},{4,5},{5,6},{6,7},{7,0},{8,9},{9,10},{10,1... | collective-permute-start | bytes 884744 | tf_op jit(solution)/shard_map/ppermute | solution.py:48
  416.2 7.9 %collective-permute-start.3 = (f32[288,256]{1,0:T(8,128)S(1)}, f32[288,256]{1,0:T(8,128)S(1)}, u32[]{:S(2)}, u32[]{:S(2)}) collective-permute-start(f32[288,256]{1,0:T(8,128)S(1)} %collective-permute-done.2), channel_id=1, source_target_pairs={{0,1},{1,2},{2,3},{3,4},{4,5},{5,6},{6,7},{7,0},{8,9},{9,10},{10,1... | collective-permute-start | bytes 884744 | tf_op jit(solution)/shard_map/ppermute | solution.py:48
  424.1 0.7 copy-start.3
  424.9 7.9 %collective-permute-start.4 = (f32[288,256]{1,0:T(8,128)S(1)}, f32[288,256]{1,0:T(8,128)S(1)}, u32[]{:S(2)}, u32[]{:S(2)}) collective-permute-start(f32[288,256]{1,0:T(8,128)S(1)} %collective-permute-done.3), channel_id=1, source_target_pairs={{0,1},{1,2},{2,3},{3,4},{4,5},{5,6},{6,7},{7,0},{8,9},{9,10},{10,1... | collective-permute-start | bytes 884744 | tf_op jit(solution)/shard_map/ppermute | solution.py:48
  432.8 0.7 copy-start.5
  433.5 8.1 %collective-permute-start.5 = (f32[288,256]{1,0:T(8,128)S(1)}, f32[288,256]{1,0:T(8,128)}, u32[]{:S(2)}, u32[]{:S(2)}) collective-permute-start(f32[288,256]{1,0:T(8,128)S(1)} %collective-permute-done.4), channel_id=1, source_target_pairs={{0,1},{1,2},{2,3},{3,4},{4,5},{5,6},{6,7},{7,0},{8,9},{9,10},{10,1... | collective-permute-start | bytes 884744 | tf_op jit(solution)/shard_map/ppermute | solution.py:48
  441.6 8.3 %collective-permute-start.6 = (f32[288,256]{1,0:T(8,128)}, f32[288,256]{1,0:T(8,128)}, u32[]{:S(2)}, u32[]{:S(2)}) collective-permute-start(f32[288,256]{1,0:T(8,128)} %collective-permute-done.5), channel_id=1, source_target_pairs={{0,1},{1,2},{2,3},{3,4},{4,5},{5,6},{6,7},{7,0},{8,9},{9,10},{10,1... | collective-permute-start | bytes 884744 | tf_op jit(solution)/shard_map/ppermute | solution.py:48
  441.6 14.3 %copy-start.6 = (f32[288,256]{1,0:T(8,128)S(1)}, f32[288,256]{1,0:T(8,128)}, u32[]{:S(2)}) copy-start(f32[288,256]{1,0:T(8,128)} %copy-done.5) | copy-start | bytes 884740
  441.6 14.3 %copy-start.4 = (f32[288,256]{1,0:T(8,128)S(1)}, f32[288,256]{1,0:T(8,128)}, u32[]{:S(2)}) copy-start(f32[288,256]{1,0:T(8,128)} %copy-done.3) | copy-start | bytes 884740
Sparse Core Ops, SparseCore 0:
  9.6 34.1 all-gather.1
  66.8 73.0 all-reduce.4
  147.1 55.4 all-reduce.6
  310.0 36.0 reduce-scatter.1
  349.0 42.2 all-reduce.8
